TPU v7x, 256 devices: a whole 4x4x8 slice. The times are simulated.
256 devices in a mesh: pop: 16 (over y, z_hi, core), col: 16 (over z_lo, x).
Axes of the slice: x: 4, y: 4, z: 8 (z_hi: 2, z_lo: 4; z = z_hi * 4 + z_lo), core: 2. Of those that a mesh axis runs over, the one named last changes fastest.
Arguments:
- tokens: bfloat16 [14336, 4096], P('pop'), may hold values from -6 to 6
- weight: bfloat16 [4096, 16384], P(None, ('col', 'pop')), may hold values from -0.09375 to 0.09375
- old_left: bfloat16 [1792, 4, 4096], P('pop', None, 'col'), may hold values from -6 to 6
- old_right: bfloat16 [1792, 4, 16384], P('pop', None, 'col'), may hold values from -6 to 6
- selected: int32 [16, 8], P('pop'), may hold values from 0 to 111, as said below
- shaping: float32 [16, 8], P('pop'), may hold values from -3 to 3
- new_left: bfloat16 [1792, 4, 4096], P('pop', None, 'col'), may hold values from -6 to 6
- new_right: bfloat16 [1792, 4, 16384], P('pop', None, 'col'), may hold values from -6 to 6
Outputs:
- updated: bfloat16 [4096, 16384], P(None, ('col', 'pop'))
- activations: bfloat16 [14336, 16384], P('pop', 'col')
Inputs may be any that keep to these rules, and one draw needn't show every extreme that they name: `selected`: each row names 8 different members of its group.
All inputs are finite; a program needn't handle non-finite values.
Results may differ from a plain program's by a relative error of at most 0.0055.
Values may be sent and summed in bfloat16 or wider, within the bound.
A program may use at most 128 MiB of HBM per device.

v0:
```python
import math
import jax
import jax.numpy as jnp
from jax import lax
from jax.sharding import PartitionSpec as P

D = 4096
RANK = 4
noise_scale = 0.5


def laid_out(parts, dim):
    parts = jnp.moveaxis(parts, 0, dim)
    lengths = parts.shape
    return parts.reshape(*lengths[:dim], lengths[dim] * lengths[dim + 1], *lengths[dim + 2 :])


def copy_for_each(x, axis):
    count = lax.axis_size(axis)
    return lax.all_to_all(jnp.broadcast_to(x[None], (count, *x.shape)), axis, 0, 0, tiled=True)


def gather_directly(x, axis, dim):
    return laid_out(copy_for_each(x, axis), dim)


def taken_together(x, axis):
    return copy_for_each(x, axis).sum(axis=0)


def contract_members(left_rows, right_rows):
    return lax.dot_general(
        left_rows, right_rows, (((0,), (0,)), ((), ())), preferred_element_type=jnp.float32
    )


def local(tokens, weight, old_left, old_right, selected, shaping, new_left, new_right):
    groups = lax.axis_size("pop")
    picked = selected[0]
    count = picked.shape[0]
    factor = 1.0 / math.sqrt(D * RANK * count * groups)
    weights_here = shaping[0] * factor
    chosen_left = jnp.take(old_left, picked, axis=0)
    chosen_right = jnp.take(old_right, picked, axis=0)
    scaled_local = (chosen_left.astype(jnp.float32) * weights_here[:, None, None]).astype(
        jnp.bfloat16
    )
    scaled_left = gather_directly(scaled_local, "col", 2)
    every_left = lax.all_gather(scaled_left, "pop", axis=0, tiled=True)
    narrow_right = lax.all_to_all(chosen_right, "pop", split_axis=2, concat_axis=0, tiled=True)
    delta = contract_members(
        every_left.reshape(-1, D), narrow_right.reshape(-1, narrow_right.shape[2])
    )
    updated = (weight.astype(jnp.float32) + delta).astype(jnp.bfloat16)
    base = jnp.dot(
        tokens,
        lax.all_gather(updated, "pop", axis=1, tiled=True),
        preferred_element_type=jnp.float32,
    )
    members_here = new_left.shape[0]
    slab = new_left.shape[2]
    offset = lax.axis_index("col") * slab
    token_slab = lax.dynamic_slice_in_dim(tokens, offset, slab, 1).reshape(members_here, -1, slab)
    partial_proj = jnp.einsum(
        "mtd,mrd->mtr", token_slab, new_left, preferred_element_type=jnp.float32
    )
    proj = taken_together(partial_proj, "col").astype(jnp.bfloat16)
    side = jnp.einsum("mtr,mrh->mth", proj, new_right, preferred_element_type=jnp.float32).reshape(
        base.shape
    )
    pre = base + noise_scale / math.sqrt(D * RANK) * side
    return (updated, (jnp.maximum(pre, 0.0) ** 2).astype(jnp.bfloat16))


def solution(mesh):
    placed = (
        P("pop", None),
        P(None, ("col", "pop")),
        P("pop", None, "col"),
        P("pop", None, "col"),
        P("pop", None),
        P("pop", None),
        P("pop", None, "col"),
        P("pop", None, "col"),
    )
    return jax.shard_map(
        local,
        mesh=mesh,
        in_specs=placed,
        out_specs=(P(None, ("col", "pop")), P("pop", "col")),
        check_vma=False,
    )
```

profile of v0, /device:TPU:1, one launch (start us, length us, event | category | flops | bytes accessed | tf_op | source)
XLA Modules:
  0.0 255.4 jit_solution(2421390312344441921)
XLA Ops:
  7.2 0.0 copy-start
  7.2 0.0 all-gather.3.cloned.1.call-start
  7.2 0.7 fusion.7
  8.0 0.7 compare_and_fusion
  8.6 0.7 multiply_bitcast_fusion.1
  9.3 1.5 gather_fusion
  10.8 0.1 multiply_convert_fusion
  10.9 18.4 %all_to_all.25 = bf16[16,8,4,256]{3,1,2,0:T(8,128)(2,1)S(1)} all-to-all(bf16[16,8,4,256]{3,1,2,0:T(8,128)(2,1)S(1)} %broadcast_in_dim.35), channel_id=1, replica_groups=mesh['pop'=16,'col'=16] {'col'}, dimensions={0} | all-to-all | bytes 524288 | tf_op jit(solution)/shard_map/all_to_all | solution.py:20
  29.3 0.7 copy.63
  30.0 0.0 all-gather.3.cloned.1.call-update
  30.0 0.0 all-gather.5.cloned.1.call-start
  30.1 1.8 gather_fusion.1
  31.9 0.1 broadcast_select_fusion
  32.0 0.7 copy.57
  32.7 1.1 reshape.88
  33.8 20.4 %all_to_all.26 = bf16[16,2,1024]{2,1,0:T(2,128)(2,1)S(1)} all-to-all(bf16[16,2,1024]{2,1,0:T(2,128)(2,1)S(1)} %reshape.88), channel_id=1, replica_groups=mesh['pop'=16,'col'=16] {'pop'}, dimensions={0} | all-to-all | bytes 131072 | tf_op jit(solution)/shard_map/all_to_all | solution.py:50
  54.2 1.2 reshape.89
  55.4 0.5 copy.58
  56.0 52.5 %all-gather.3.cloned.1.call-done = bf16[128,4,4096]{2,0,1:T(8,128)(2,1)} async-done(((bf16[8,4,4096]{2,0,1:T(8,128)(2,1)}), bf16[128,4,4096]{2,0,1:T(8,128)(2,1)}) %all-gather.3.cloned.1.call-update) | async-done | bytes 4194320 | tf_op jit(solution)/shard_map/all_gather | solution.py:49
  108.5 7.4 %copy.56 = bf16[128,4,4096]{2,1,0:T(4,128)(2,1)} copy(bf16[128,4,4096]{2,0,1:T(8,128)(2,1)} %all-gather.3.cloned.1.call-done) | data formatting | bytes 8388608 | tf_op jit(solution)/shard_map/all_gather | solution.py:49
  115.9 0.0 copy-start.1
  115.9 7.0 %reshape.69 = bf16[512,4096]{1,0:T(8,128)(2,1)} reshape(bf16[128,4,4096]{2,1,0:T(4,128)(2,1)} %copy.56) | data formatting | bytes 8388608 | tf_op jit(solution)/shard_map/reshape | solution.py:52
  122.9 0.0 copy-start.2
  122.9 0.0 copy-done.1
  122.9 3.9 %fusion = bf16[4096,64]{0,1:T(8,128)(2,1)} fusion(bf16[512,4096]{1,0:T(8,128)(2,1)} %reshape.69, bf16[512,64]{1,0:T(8,128)(2,1)S(1)} %bitcast.41, bf16[4096,64]{0,1:T(8,128)(2,1)S(1)} %copy-done.1), kind=kOutput, calls=%fused_computation.3 | convolution fusion | flops 269221888 | bytes 5308416 | tf_op jit(solution)/shard_map/dot_general | solution.py:32
  126.8 0.0 all-gather.5.cloned.1.call-update
  126.8 0.0 copy-done.2
  126.8 1.3 fusion.4
  128.1 0.1 copy.59
  128.2 0.1 broadcast_in_dim.38
  128.3 14.1 %all_to_all.27 = f32[16,112,8,4]{1,2,3,0:T(8,128)S(1)} all-to-all(f32[16,112,8,4]{1,2,3,0:T(8,128)S(1)} %broadcast_in_dim.38), channel_id=1, replica_groups=mesh['pop'=16,'col'=16] {'col'}, dimensions={0} | all-to-all | bytes 458752 | tf_op jit(solution)/shard_map/all_to_all | solution.py:20
  142.4 0.2 copy.60
  142.6 0.0 copy-done
  142.6 2.6 %multiply_bitcast_fusion = f32[896,1024]{1,0:T(8,128)} fusion(bf16[112,8,4]{1,2,0:T(4,128)(2,1)S(1)} %copy.60, bf16[112,4,1024]{2,1,0:T(4,128)(2,1)S(1)} %copy-done), kind=kOutput, calls=%fused_computation.8 | convolution fusion | flops 8257536 | bytes 4594688 | tf_op jit(solution)/shard_map/mtr,mrh->mth/dot_general | solution.py:68
  145.1 5.0 %copy.61 = f32[896,1024]{0,1:T(8,128)} copy(f32[896,1024]{1,0:T(8,128)} %multiply_bitcast_fusion) | data formatting | bytes 7340032 | tf_op jit(solution)/shard_map/mul | solution.py:71
  150.1 81.9 %all-gather.5.cloned.1.call-done = bf16[4096,1024]{0,1:T(8,128)(2,1)} async-done(((bf16[4096,64]{0,1:T(8,128)(2,1)}), bf16[4096,1024]{0,1:T(8,128)(2,1)}) %all-gather.5.cloned.1.call-update) | async-done | bytes 8388624 | tf_op jit(solution)/shard_map/all_gather | solution.py:57
  232.1 14.0 %fusion.3 = bf16[896,1024]{0,1:T(8,128)(2,1)S(1)} fusion(f32[896,1024]{0,1:T(8,128)} %copy.61, bf16[4096,1024]{0,1:T(8,128)(2,1)} %all-gather.5.cloned.1.call-done, bf16[896,4096]{1,0:T(8,128)(2,1)} %param.8), kind=kOutput, calls=%fused_computation.7 | convolution fusion | flops 7519862784 | bytes 21233664 | tf_op jit(solution)/shard_map/dot_general | solution.py:55
  246.1 2.4 copy.62
  (3 shorter events, 0.1 us)
Async XLA Ops:
  7.2 135.4 %copy-start = (bf16[112,4,1024]{2,1,0:T(4,128)(2,1)S(1)}, bf16[112,4,1024]{2,1,0:T(4,128)(2,1)}, u32[]{:S(2)}) copy-start(bf16[112,4,1024]{2,1,0:T(4,128)(2,1)} %param.15) | copy-start | bytes 2752516
  7.2 101.3 %all-gather.3.cloned.1.call-start = ((), (), s32[]{:S(2)}) async-start(), calls=%async_computation.3 | async-start | bytes 4456448 | tf_op jit(solution)/shard_map/all_gather | solution.py:49
  30.0 202.1 %all-gather.5.cloned.1.call-start = ((), (), s32[]{:S(2)}) async-start(), calls=%async_computation.4 | async-start | bytes 8912896 | tf_op jit(solution)/shard_map/all_gather | solution.py:57
  115.9 7.0 %copy-start.1 = (bf16[4096,64]{0,1:T(8,128)(2,1)S(1)}, bf16[4096,64]{0,1:T(8,128)(2,1)}, u32[]{:S(2)}) copy-start(bf16[4096,64]{0,1:T(8,128)(2,1)} %param.9) | copy-start | bytes 1572868
  122.9 3.9 %copy-start.2 = (bf16[112,4,256]{2,1,0:T(4,128)(2,1)S(1)}, bf16[112,4,256]{2,1,0:T(4,128)(2,1)}, u32[]{:S(2)}) copy-start(bf16[112,4,256]{2,1,0:T(4,128)(2,1)} %param.14) | copy-start | bytes 688132
Sparse Core Ops, SparseCore 0:
  30.2 78.3 all-gather.2
  127.0 105.0 all-gather.4
where the time goes:
time: 256 us; the launch traced here: 255 us
  waiting for transfers between devices  135 us (53%)
  blocking collectives  52.9 us (21%)
  local copies, waits for them, and re-layouts  29.7 us (12%)
  matrix products  21.8 us (9%)
  between operations  14.1 us (6%)
    all_gather x1, waiting for transfers between devices, local(): lax.all_gather(updated, 'pop', axis=1, tiled=True)  81.9 us
    all_gather x1, waiting for transfers between devices, local(): every_left = lax.all_gather(scaled_left, 'pop', axis=0, tiled=True)  52.5 us
    all_to_all x2, blocking collectives, copy_for_each(): lax.all_to_all(jnp.broadcast_to(x[None], (count, *x.shape)), axis, 0, 0,...  32.5 us
    all_to_all x1, blocking collectives, local(): lax.all_to_all(chosen_right, 'pop', split_axis=2, concat_axis=0, tiled=True)  20.4 us
    dot_general x1, matrix products, local(): jnp.dot(tokens, lax.all_gather(updated, 'pop', axis=1, tiled=True), prefe...  14 us
    all_gather x1, local copies, waits for them, and re-layouts, local(): every_left = lax.all_gather(scaled_left, 'pop', axis=0, tiled=True)  7.37 us
    reshape x1, local copies, waits for them, and re-layouts, local(): every_left.reshape(-1, D)  7 us
  transfers between devices with their start and end apart: 2, of which 2 were waited for; matrix products, arithmetic and copies ran while one was open for 6% of the time, Pallas kernels for 0%

commit v1 on v0

--- a/solution.py
+++ b/solution.py
@@ -47,7 +47,10 @@
     )
     scaled_left = gather_directly(scaled_local, "col", 2)
     every_left = lax.all_gather(scaled_left, "pop", axis=0, tiled=True)
-    narrow_right = lax.all_to_all(chosen_right, "pop", split_axis=2, concat_axis=0, tiled=True)
+    size = lax.axis_size("pop")
+    blocks = jnp.stack(jnp.split(chosen_right, size, axis=2), axis=0)
+    blocks = lax.all_to_all(blocks, "pop", split_axis=0, concat_axis=0)
+    narrow_right = jnp.concatenate(blocks, axis=0)
     delta = contract_members(
         every_left.reshape(-1, D), narrow_right.reshape(-1, narrow_right.shape[2])
     )

time: 256 us -> 255 us (level)
  transfers between devices with their start and end apart: 2 -> 2, of which waited for: 2 -> 2; matrix products, arithmetic and copies ran while one was open for 6% -> 5% of each run, Pallas kernels for 0% -> 0%
where the time goes in v1:
time: 255 us
  waiting for transfers between devices  137 us (54%)
  blocking collectives  52.8 us (21%)
  local copies, waits for them, and re-layouts  27.2 us (11%)
  matrix products  21.8 us (9%)
  between operations  14.2 us (6%)
    all_gather x1, waiting for transfers between devices, local(): lax.all_gather(updated, 'pop', axis=1, tiled=True)  81.9 us
    all_gather x1, waiting for transfers between devices, local(): every_left = lax.all_gather(scaled_left, 'pop', axis=0, tiled=True)  54.6 us
    all_to_all x2, blocking collectives, copy_for_each(): lax.all_to_all(jnp.broadcast_to(x[None], (count, *x.shape)), axis, 0, 0,...  32.5 us
    all_to_all x1, blocking collectives, local(): blocks = lax.all_to_all(blocks, 'pop', split_axis=0, concat_axis=0)  20.3 us
    dot_general x1, matrix products, local(): jnp.dot(tokens, lax.all_gather(updated, 'pop', axis=1, tiled=True), prefe...  14 us
    all_gather x1, local copies, waits for them, and re-layouts, local(): every_left = lax.all_gather(scaled_left, 'pop', axis=0, tiled=True)  7.37 us
    reshape x1, local copies, waits for them, and re-layouts, local(): every_left.reshape(-1, D)  7 us
  transfers between devices with their start and end apart: 2, of which 2 were waited for; matrix products, arithmetic and copies ran while one was open for 5% of the time, Pallas kernels for 0%

profile of v1, /device:TPU:1, one launch (start us, length us, event | category | flops | bytes accessed | tf_op | source)
XLA Modules:
  0.0 254.8 jit_solution(9738623920727268595)
XLA Ops:
  7.2 0.0 copy-start
  7.2 0.0 all-gather.3.cloned.1.call-start
  7.2 0.7 fusion.7
  8.0 0.7 compare_and_fusion
  8.6 0.7 multiply_bitcast_fusion.1
  9.3 1.5 gather_fusion
  10.8 0.1 multiply_convert_fusion
  10.9 18.4 %all_to_all.15 = bf16[16,8,4,256]{3,1,2,0:T(8,128)(2,1)S(1)} all-to-all(bf16[16,8,4,256]{3,1,2,0:T(8,128)(2,1)S(1)} %broadcast_in_dim.35), channel_id=1, replica_groups=mesh['pop'=16,'col'=16] {'col'}, dimensions={0} | all-to-all | bytes 524288 | tf_op jit(solution)/shard_map/all_to_all | solution.py:20
  29.3 0.7 copy.46
  30.0 0.0 all-gather.3.cloned.1.call-update
  30.0 0.0 all-gather.5.cloned.1.call-start
  30.1 1.8 gather_fusion.1
  31.9 0.1 broadcast_select_fusion
  32.0 0.1 constant_dynamic-update-slice_fusion.14
  32.1 0.1 constant_dynamic-update-slice_fusion.12
  32.2 0.1 constant_dynamic-update-slice_fusion.10
  32.3 0.1 constant_dynamic-update-slice_fusion.8
  32.4 0.1 constant_dynamic-update-slice_fusion.6
  32.5 0.1 constant_dynamic-update-slice_fusion.4
  32.6 0.1 constant_dynamic-update-slice_fusion.2
  32.7 0.1 constant_dynamic-update-slice_fusion
  32.8 0.1 reshape.83
  32.9 20.3 %all_to_all.16 = bf16[16,2,1024]{2,1,0:T(2,128)(2,1)S(1)} all-to-all(bf16[16,2,1024]{2,1,0:T(2,128)(2,1)S(1)} %reshape.83), channel_id=1, replica_groups=mesh['pop'=16,'col'=16] {'pop'}, dimensions={0} | all-to-all | bytes 131072 | tf_op jit(solution)/shard_map/all_to_all | solution.py:52
  53.2 0.1 reshape.84
  53.4 54.6 %all-gather.3.cloned.1.call-done = bf16[128,4,4096]{2,0,1:T(8,128)(2,1)} async-done(((bf16[8,4,4096]{2,0,1:T(8,128)(2,1)}), bf16[128,4,4096]{2,0,1:T(8,128)(2,1)}) %all-gather.3.cloned.1.call-update) | async-done | bytes 4194320 | tf_op jit(solution)/shard_map/all_gather | solution.py:49
  108.0 7.4 %copy.41 = bf16[128,4,4096]{2,1,0:T(4,128)(2,1)} copy(bf16[128,4,4096]{2,0,1:T(8,128)(2,1)} %all-gather.3.cloned.1.call-done) | data formatting | bytes 8388608 | tf_op jit(solution)/shard_map/all_gather | solution.py:49
  115.3 0.0 copy-start.1
  115.3 7.0 %reshape.65 = bf16[512,4096]{1,0:T(8,128)(2,1)} reshape(bf16[128,4,4096]{2,1,0:T(4,128)(2,1)} %copy.41) | data formatting | bytes 8388608 | tf_op jit(solution)/shard_map/reshape | solution.py:55
  122.3 0.0 copy-start.2
  122.3 0.0 copy-done.1
  122.3 3.9 %fusion = bf16[4096,64]{0,1:T(8,128)(2,1)} fusion(bf16[512,4096]{1,0:T(8,128)(2,1)} %reshape.65, bf16[512,64]{1,0:T(8,128)(2,1)S(1)} %bitcast.98, bf16[4096,64]{0,1:T(8,128)(2,1)S(1)} %copy-done.1), kind=kOutput, calls=%fused_computation.3 | convolution fusion | flops 269221888 | bytes 5308416 | tf_op jit(solution)/shard_map/dot_general | solution.py:32
  126.3 0.0 all-gather.5.cloned.1.call-update
  126.3 0.0 copy-done.2
  126.3 1.3 fusion.4
  127.6 0.1 copy.42
  127.7 0.1 broadcast_in_dim.38
  127.7 14.1 %all_to_all.17 = f32[16,112,8,4]{1,2,3,0:T(8,128)S(1)} all-to-all(f32[16,112,8,4]{1,2,3,0:T(8,128)S(1)} %broadcast_in_dim.38), channel_id=1, replica_groups=mesh['pop'=16,'col'=16] {'col'}, dimensions={0} | all-to-all | bytes 458752 | tf_op jit(solution)/shard_map/all_to_all | solution.py:20
  141.8 0.2 copy.43
  142.0 0.0 copy-done
  142.0 2.6 %multiply_bitcast_fusion = f32[896,1024]{1,0:T(8,128)} fusion(bf16[112,8,4]{1,2,0:T(4,128)(2,1)S(1)} %copy.43, bf16[112,4,1024]{2,1,0:T(4,128)(2,1)S(1)} %copy-done), kind=kOutput, calls=%fused_computation.8 | convolution fusion | flops 8257536 | bytes 4594688 | tf_op jit(solution)/shard_map/mtr,mrh->mth/dot_general | solution.py:71
  144.6 5.0 %copy.44 = f32[896,1024]{0,1:T(8,128)} copy(f32[896,1024]{1,0:T(8,128)} %multiply_bitcast_fusion) | data formatting | bytes 7340032 | tf_op jit(solution)/shard_map/mul | solution.py:74
  149.6 81.9 %all-gather.5.cloned.1.call-done = bf16[4096,1024]{0,1:T(8,128)(2,1)} async-done(((bf16[4096,64]{0,1:T(8,128)(2,1)}), bf16[4096,1024]{0,1:T(8,128)(2,1)}) %all-gather.5.cloned.1.call-update) | async-done | bytes 8388624 | tf_op jit(solution)/shard_map/all_gather | solution.py:60
  231.5 14.0 %fusion.3 = bf16[896,1024]{0,1:T(8,128)(2,1)S(1)} fusion(f32[896,1024]{0,1:T(8,128)} %copy.44, bf16[4096,1024]{0,1:T(8,128)(2,1)} %all-gather.5.cloned.1.call-done, bf16[896,4096]{1,0:T(8,128)(2,1)} %param.8), kind=kOutput, calls=%fused_computation.7 | convolution fusion | flops 7519862784 | bytes 21233664 | tf_op jit(solution)/shard_map/dot_general | solution.py:58
  245.6 2.4 copy.45
  (11 shorter events, 0.2 us)
Async XLA Ops:
  7.2 134.8 %copy-start = (bf16[112,4,1024]{2,1,0:T(4,128)(2,1)S(1)}, bf16[112,4,1024]{2,1,0:T(4,128)(2,1)}, u32[]{:S(2)}) copy-start(bf16[112,4,1024]{2,1,0:T(4,128)(2,1)} %param.15) | copy-start | bytes 2752516
  7.2 100.8 %all-gather.3.cloned.1.call-start = ((), (), s32[]{:S(2)}) async-start(), calls=%async_computation.3 | async-start | bytes 4456448 | tf_op jit(solution)/shard_map/all_gather | solution.py:49
  30.0 201.5 %all-gather.5.cloned.1.call-start = ((), (), s32[]{:S(2)}) async-start(), calls=%async_computation.4 | async-start | bytes 8912896 | tf_op jit(solution)/shard_map/all_gather | solution.py:60
  115.3 7.0 %copy-start.1 = (bf16[4096,64]{0,1:T(8,128)(2,1)S(1)}, bf16[4096,64]{0,1:T(8,128)(2,1)}, u32[]{:S(2)}) copy-start(bf16[4096,64]{0,1:T(8,128)(2,1)} %param.9) | copy-start | bytes 1572868
  122.3 3.9 %copy-start.2 = (bf16[112,4,256]{2,1,0:T(4,128)(2,1)S(1)}, bf16[112,4,256]{2,1,0:T(4,128)(2,1)}, u32[]{:S(2)}) copy-start(bf16[112,4,256]{2,1,0:T(4,128)(2,1)} %param.14) | copy-start | bytes 688132
Sparse Core Ops, SparseCore 0:
  30.2 77.7 all-gather.2
  126.4 105.0 all-gather.4
